TPU v7x, 32 devices: a whole 2x2x4 slice. The times are simulated.
32 devices in a mesh: rows: 4 (over y, x), cols: 8 (over z, core).
Axes of the slice: x: 2, y: 2, z: 4, core: 2. Of those that a mesh axis runs over, the one named last changes fastest.
Arguments:
- latent1: bfloat16 [64, 512, 320], P('rows', 'cols'), may hold values from -15 to 15, as said below
- norm1a_g: float32 [320], replicated, may hold values from 0.25 to 1.75
- norm1a_b: float32 [320], replicated, may hold values from -3 to 3
- conv1a_w: bfloat16 [3, 3, 320, 320], replicated, may hold values from -0.109375 to 0.109375
- norm1b_g: float32 [320], replicated, may hold values from 0.25 to 1.75
- norm1b_b: float32 [320], replicated, may hold values from -3 to 3
- conv1b_w: bfloat16 [3, 3, 320, 320], replicated, may hold values from -0.109375 to 0.109375
- conv1b_b: float32 [320], replicated, may hold values from -3 to 3
- feat3: bfloat16 [16, 128, 1280], P('rows', 'cols'), may hold values from -15 to 15, as said below
- adapter3: bfloat16 [16, 128, 1280], P('rows', 'cols'), may hold values from -15 to 15, as said below
- norm3a_g: float32 [1280], replicated, may hold values from 0.25 to 1.75
- norm3a_b: float32 [1280], replicated, may hold values from -3 to 3
- conv3a_w: bfloat16 [3, 3, 1280, 1280], P(None, None, None, 'cols'), may hold values from -0.0546875 to 0.0546875
- norm3b_g: float32 [1280], P('cols'), may hold values from 0.25 to 1.75
- norm3b_b: float32 [1280], P('cols'), may hold values from -3 to 3
- conv3b_w: bfloat16 [3, 3, 1280, 1280], P(None, None, None, 'cols'), may hold values from -0.0546875 to 0.0546875
- conv3b_b: float32 [1280], P('cols'), may hold values from -3 to 3
Outputs:
- out1: bfloat16 [64, 512, 320], P('rows', 'cols')
- out3: bfloat16 [16, 128, 1280], P('rows', None, 'cols')
Inputs may be any that keep to these rules, and one draw needn't show every extreme that they name: `latent1`: real values. `feat3`: real values. `adapter3`: real values.
All inputs are finite; a program needn't handle non-finite values.
Results may differ from a plain program's by a relative error of at most 0.0052.
Values may be sent and summed in bfloat16 or wider, within the bound.
No kernel may reach another device: no remote copies, remote signals or barrier semaphores. Data moves between devices by JAX's collectives and lax.ppermute only.
A program may use at most 128 MiB of HBM per device.

v0:
```python
import jax
import jax.numpy as jnp
from jax import lax
from jax.sharding import PartitionSpec as P

C1 = 320
C3 = 1280
norm_eps = 1e-05


def extended(block, sides, width):
    for axis, dim in sides:
        count = lax.axis_size(axis)
        forward = [(i, i + 1) for i in range(count - 1)]
        backward = [(target, source) for source, target in forward]
        low = lax.ppermute(
            lax.slice_in_dim(block, block.shape[dim] - width, None, axis=dim), axis, forward
        )
        high = lax.ppermute(lax.slice_in_dim(block, 0, width, axis=dim), axis, backward)
        block = jnp.concatenate([low, block, high], axis=dim)
    return block


def conv_valid(padded, kernel):
    return lax.conv_general_dilated(
        padded[None],
        kernel,
        (1, 1),
        "VALID",
        dimension_numbers=("NHWC", "HWIO", "NHWC"),
        preferred_element_type=jnp.float32,
    )[0]


def moments(value, group_width):
    height, width, chans = value.shape
    grouped = value.astype(jnp.float32).reshape(height, width, chans // group_width, group_width)
    return (jnp.sum(grouped, axis=(0, 1, 3)), jnp.sum(grouped * grouped, axis=(0, 1, 3)))


def normalize(value, sums, squares, count, gain, shift):
    height, width, chans = value.shape
    groups = sums.shape[0]
    mean = sums / count
    inverse = lax.rsqrt(squares / count - mean * mean + norm_eps)
    grouped = value.astype(jnp.float32).reshape(height, width, groups, chans // groups)
    normed = ((grouped - mean[:, None]) * inverse[:, None]).reshape(height, width, chans)
    return jax.nn.silu(normed * gain + shift).astype(jnp.bfloat16)


def level3_totals(values, group_width):
    sums, squares = moments(values, group_width)
    return lax.psum((sums, squares), "rows")


def folder(kernel, total, piece):
    height = total.shape[0]
    width = total.shape[1]
    count = piece.shape[2]
    wide = jnp.pad(piece, ((0, 0), (1, 1), (0, 0)))
    taps = [wide[dy : dy + height, dx : dx + width, :] for dy in range(3) for dx in range(3)]
    patches = jnp.concatenate(taps, axis=2).reshape(height * width, 9 * count)
    weights = kernel.reshape(9 * count, kernel.shape[3])
    product = jnp.dot(patches, weights, preferred_element_type=jnp.float32)
    return product.reshape(height, width, kernel.shape[3])


def body(
    latent1,
    norm1a_g,
    norm1a_b,
    conv1a_w,
    norm1b_g,
    norm1b_b,
    conv1b_w,
    conv1b_b,
    feat3,
    adapter3,
    norm3a_g,
    norm3a_b,
    conv3a_w,
    norm3b_g,
    norm3b_b,
    conv3b_w,
    conv3b_b,
):
    rows_one = latent1.shape[0]
    cols_one = latent1.shape[1]
    width_one = C1 // 32
    count_one = rows_one * cols_one * lax.axis_size("rows") * lax.axis_size("cols") * width_one
    sums, squares = moments(latent1, width_one)
    sums, squares = lax.psum((sums, squares), ("rows", "cols"))
    act1 = normalize(latent1, sums, squares, count_one, norm1a_g, norm1a_b)
    padded = extended(act1, (("rows", 0), ("cols", 1)), 1)
    hid1 = conv_valid(padded, conv1a_w)
    sums_two, squares_two = moments(hid1, width_one)
    sums_two, squares_two = lax.psum((sums_two, squares_two), ("rows", "cols"))
    act2 = normalize(hid1, sums_two, squares_two, count_one, norm1b_g, norm1b_b)
    padded_two = extended(act2, (("rows", 0), ("cols", 1)), 1)
    out1 = (latent1.astype(jnp.float32) + conv_valid(padded_two, conv1b_w) + conv1b_b).astype(
        jnp.bfloat16
    )
    joined = (feat3.astype(jnp.float32) + adapter3.astype(jnp.float32)).astype(jnp.bfloat16)
    shard = conv3a_w.shape[3]
    height = feat3.shape[0]
    width = feat3.shape[1] * lax.axis_size("cols")
    width_three = C3 // 32
    count_three = height * width * lax.axis_size("rows") * width_three
    empty = jnp.zeros((height, width, shard), jnp.float32)
    edged_tile = extended(joined, (("rows", 0),), 1)
    whole = lax.all_gather(edged_tile, "cols", axis=1, tiled=True)
    local = lax.dynamic_slice_in_dim(whole[1:-1], lax.axis_index("cols") * shard, shard, 2)
    sums_three, squares_three = level3_totals(whole[1:-1], width_three)
    line_ids = lax.axis_index("rows") * height - 1 + jnp.arange(height + 2, dtype=jnp.int32)
    line_ok = (line_ids >= 0) & (line_ids < height * lax.axis_size("rows"))
    act_whole = normalize(whole, sums_three, squares_three, count_three, norm3a_g, norm3a_b)
    act_whole = jnp.where(line_ok[:, None, None], act_whole, jnp.zeros((), jnp.bfloat16))
    hid3 = conv_valid(jnp.pad(act_whole, ((0, 0), (1, 1), (0, 0))), conv3a_w)
    sums_four, squares_four = moments(hid3, width_three)
    sums_four, squares_four = lax.psum((sums_four, squares_four), "rows")
    act4 = normalize(hid3, sums_four, squares_four, count_three, norm3b_g, norm3b_b)
    edged_two = extended(act4, (("rows", 0),), 1)
    second = folder(conv3b_w, empty, lax.all_gather(edged_two, "cols", axis=2, tiled=True))
    out3 = (local.astype(jnp.float32) + second + conv3b_b).astype(jnp.bfloat16)
    return (out1, out3)


def solution(mesh):
    placed = (
        P("rows", "cols", None),
        P(),
        P(),
        P(),
        P(),
        P(),
        P(),
        P(),
        P("rows", "cols", None),
        P("rows", "cols", None),
        P(),
        P(),
        P(None, None, None, "cols"),
        P("cols"),
        P("cols"),
        P(None, None, None, "cols"),
        P("cols"),
    )
    return jax.shard_map(
        body,
        mesh=mesh,
        in_specs=placed,
        out_specs=(P("rows", "cols", None), P("rows", None, "cols")),
        check_vma=False,
    )
```

profile of v0, /device:TPU:3, one launch (start us, length us, event | category | flops | bytes accessed | tf_op | source)
XLA Modules:
  0.0 271.7 jit_solution(1989159942951387046)
XLA Ops:
  8.4 3.1 %collective-permute-start.8 = (bf16[1,16,1280]{2,1,0:T(8,128)(2,1)S(1)}, bf16[1,16,1280]{2,1,0:T(8,128)(2,1)S(1)}, u32[]{:S(2)}, u32[]{:S(2)}) collective-permute-start(bf16[1,16,1280]{2,1,0:T(8,128)(2,1)S(1)} %get-tuple-element.38), channel_id=1, source_target_pairs={{0,8},{8,16},{16,24},{1,9},{9,17},{17,25},{2,10},{10,18},{18,26},{... | collective-permute-start | bytes 122888 | tf_op jit(solution)/shard_map/ppermute | solution.py:16
  13.7 3.5 %collective-permute-done.9 = bf16[1,16,1280]{2,1,0:T(8,128)(2,1)S(1)} collective-permute-done((bf16[1,16,1280]{2,1,0:T(8,128)(2,1)S(1)}, bf16[1,16,1280]{2,1,0:T(8,128)(2,1)S(1)}, u32[]{:S(2)}, u32[]{:S(2)}) %collective-permute-start.9) | collective-permute-done | bytes 40992 | tf_op jit(solution)/shard_map/ppermute | solution.py:19
  21.2 27.1 %all-gather.3.cloned.1.call-done = bf16[6,128,1280]{2,1,0:T(8,128)(2,1)} async-done(((bf16[6,16,1280]{2,1,0:T(8,128)(2,1)}), bf16[6,128,1280]{2,1,0:T(8,128)(2,1)}) %all-gather.3.cloned.1.call-update) | async-done | bytes 1966096 | tf_op jit(solution)/shard_map/all_gather | solution.py:111
  53.2 6.0 %all-reduce.5 = (f32[32]{0:T(128)S(1)}, f32[32]{0:T(128)S(1)}) all-reduce(f32[32]{0:T(128)S(1)} %reduce_sum.145, f32[32]{0:T(128)S(1)} %reduce_sum.115), channel_id=1, replica_groups=mesh['rows'=4,'cols'=8] {'rows'}, use_global_device_ids=true, to_apply=%region_17.18 | all-reduce | flops 64 | bytes 512 | tf_op jit(solution)/shard_map/psum | solution.py:53
  59.5 3.0 %fusion.11 = bf16[6,128,1280]{2,1,0:T(8,128)(2,1)S(1)} fusion(bf16[6,128,1280]{2,1,0:T(8,128)(2,1)} %all-gather.3.cloned.1.call-done, f32[1280]{0:T(1024)S(1)} %copy-done.4, f32[1280]{0:T(1024)S(1)} %copy-done.5, f32[1280]{0:T(1024)S(1)} %mul.156, f32[1280]{0:T(1024)S(1)} %sub.79, pred[6]{0:T(512)(128)(4,1)S(1)} %compare_and_fusion), kind=kLoop, calls=%fused_computation.20 | loop fusion | flops 10813440 | bytes 3952646 | tf_op jit(solution)/shard_map/jit(_where)/select_n | solution.py:117
  64.5 4.2 %reshape.81 = bf16[6,1,8,17,1280]{4,3,2,0,1:T(8,128)(2,1)} reshape(bf16[6,1,136,1280]{3,2,0,1:T(8,128)(2,1)} %pad.13) | data formatting | bytes 4177920 | tf_op jit(solution)/shard_map/conv_general_dilated | solution.py:25
  71.6 3.5 %select_reduce_fusion.3 = (f32[160]{0:T(256)S(1)}, f32[160]{0:T(256)S(1)}, f32[4,8,17,160]{3,1,2,0:T(8,128)S(1)}) fusion(pred[8,17]{0,1:T(8,128)(4,1)S(1)} %copy-done.18, bf16[3,3,1280,160]{2,3,1,0:T(8,128)(2,1)S(1)} %copy-done.15, bf16[6,1,7,2,1280]{4,2,3,0,1:T(8,128)(2,1)S(1)} %slice.109, bf16[6,1,8,17,1280]{4,2,3,0,1:T(8,128)(2,1)S(1)} %copy.104), kind=kOutput, calls=%fused_computation.73 | convolution fusion | flops 2012927744 | bytes 6339976 | tf_op jit(solution)/shard_map/conv_general_dilated | solution.py:25
  75.5 42.0 %all-reduce.3 = (f32[32]{0:T(128)}, f32[32]{0:T(128)}) all-reduce(f32[32]{0:T(128)S(1)} %copy-done.11, f32[32]{0:T(128)S(1)} %copy-done.12), channel_id=1, replica_groups=mesh['rows'=4,'cols'=8] {'rows','cols'}, use_global_device_ids=true, to_apply=%region_5.6 | all-reduce | flops 64 | bytes 512 | tf_op jit(solution)/shard_map/psum | solution.py:92
  117.5 6.0 %all-reduce.4 = (f32[4]{0:T(128)S(1)}, f32[4]{0:T(128)S(1)}) all-reduce(f32[4]{0:T(128)S(1)} %reduce_sum.151, f32[4]{0:T(128)S(1)} %reduce_sum.148), channel_id=1, replica_groups=mesh['rows'=4,'cols'=8] {'rows'}, use_global_device_ids=true, to_apply=%region_23.24 | all-reduce | flops 8 | bytes 64 | tf_op jit(solution)/shard_map/psum | solution.py:120
  127.5 4.0 %collective-permute-start.10 = (bf16[1,128,160]{1,2,0:T(8,128)(2,1)S(1)}, bf16[1,128,160]{1,2,0:T(8,128)(2,1)S(1)}, u32[]{:S(2)}, u32[]{:S(2)}) collective-permute-start(bf16[1,128,160]{1,2,0:T(8,128)(2,1)S(1)} %get-tuple-element.36), channel_id=1, source_target_pairs={{0,8},{8,16},{16,24},{1,9},{9,17},{17,25},{2,10},{10,18},{18,26},{... | collective-permute-start | bytes 122888 | tf_op jit(solution)/shard_map/ppermute | solution.py:16
  133.8 3.3 %collective-permute-done.11 = bf16[1,128,160]{1,2,0:T(8,128)(2,1)S(1)} collective-permute-done((bf16[1,128,160]{1,2,0:T(8,128)(2,1)S(1)}, bf16[1,128,160]{1,2,0:T(8,128)(2,1)S(1)}, u32[]{:S(2)}, u32[]{:S(2)}) %collective-permute-start.11) | collective-permute-done | bytes 40992 | tf_op jit(solution)/shard_map/ppermute | solution.py:19
  140.8 3.4 %collective-permute-start.1 = (bf16[1,64,320]{2,0,1:T(2,128)(2,1)S(1)}, bf16[1,64,320]{2,0,1:T(2,128)(2,1)S(1)}, u32[]{:S(2)}, u32[]{:S(2)}) collective-permute-start(bf16[1,64,320]{2,0,1:T(2,128)(2,1)S(1)} %get-tuple-element.35), channel_id=1, source_target_pairs={{8,0},{16,8},{24,16},{9,1},{17,9},{25,17},{10,2},{18,10},{26,18},{... | collective-permute-start | bytes 122888 | tf_op jit(solution)/shard_map/ppermute | solution.py:19
  144.2 2.8 %collective-permute-done.1 = bf16[1,64,320]{2,0,1:T(2,128)(2,1)S(1)} collective-permute-done((bf16[1,64,320]{2,0,1:T(2,128)(2,1)S(1)}, bf16[1,64,320]{2,0,1:T(2,128)(2,1)S(1)}, u32[]{:S(2)}, u32[]{:S(2)}) %collective-permute-start.1) | collective-permute-done | bytes 40992 | tf_op jit(solution)/shard_map/ppermute | solution.py:19
  147.0 9.3 %collective-permute-start.2 = (bf16[18,1,320]{2,0,1:T(8,128)(2,1)S(1)}, bf16[18,1,320]{2,0,1:T(8,128)(2,1)S(1)}, u32[]{:S(2)}, u32[]{:S(2)}) collective-permute-start(bf16[18,1,320]{2,0,1:T(8,128)(2,1)S(1)} %get-tuple-element.30), channel_id=1, source_target_pairs={{0,1},{1,2},{2,3},{3,4},{4,5},{5,6},{6,7},{8,9},{9,10},{10,11},{11... | collective-permute-start | bytes 34568 | tf_op jit(solution)/shard_map/ppermute | solution.py:16
  158.4 4.4 %collective-permute-done.3 = bf16[18,1,320]{2,0,1:T(8,128)(2,1)S(1)} collective-permute-done((bf16[18,1,320]{2,0,1:T(8,128)(2,1)S(1)}, bf16[18,1,320]{2,0,1:T(8,128)(2,1)S(1)}, u32[]{:S(2)}, u32[]{:S(2)}) %collective-permute-start.3) | collective-permute-done | bytes 11552 | tf_op jit(solution)/shard_map/ppermute | solution.py:19
  164.2 5.1 %select_reduce_fusion.1 = (f32[320]{0:T(512)S(1)}, f32[320]{0:T(512)S(1)}, f32[16,8,9,320]{3,1,2,0:T(8,128)}) fusion(pred[8,9]{0,1:T(8,128)(4,1)S(1)} %copy-done.19, bf16[3,3,320,320]{3,2,1,0:T(8,128)(2,1)S(1)} %copy-done, bf16[18,1,7,2,320]{4,2,3,0,1:T(8,128)(2,1)S(1)} %slice.100, bf16[18,1,8,9,320]{4,2,3,0,1:T(8,128)(2,1)S(1)} %copy.97), kind=kOutput, calls=%fused_computation.22 | convolution fusion | flops 2128619008 | bytes 4311112 | tf_op jit(solution)/shard_map/conv_general_dilated | solution.py:25
  169.8 37.3 %all-reduce.2 = (f32[32]{0:T(128)S(1)}, f32[32]{0:T(128)S(1)}) all-reduce(f32[32]{0:T(128)S(1)} %reduce_sum.112, f32[32]{0:T(128)S(1)} %reduce_sum.106), channel_id=1, replica_groups=mesh['rows'=4,'cols'=8] {'rows','cols'}, use_global_device_ids=true, to_apply=%region_11.12 | all-reduce | flops 64 | bytes 512 | tf_op jit(solution)/shard_map/psum | solution.py:97
  210.0 3.1 %collective-permute-start.4 = (bf16[1,64,320]{2,0,1:T(2,128)(2,1)S(1)}, bf16[1,64,320]{2,0,1:T(2,128)(2,1)S(1)}, u32[]{:S(2)}, u32[]{:S(2)}) collective-permute-start(bf16[1,64,320]{2,0,1:T(2,128)(2,1)S(1)} %get-tuple-element.32), channel_id=1, source_target_pairs={{0,8},{8,16},{16,24},{1,9},{9,17},{17,25},{2,10},{10,18},{18,26},{... | collective-permute-start | bytes 122888 | tf_op jit(solution)/shard_map/ppermute | solution.py:16
  215.4 4.0 %collective-permute-done.5 = bf16[1,64,320]{2,0,1:T(2,128)(2,1)S(1)} collective-permute-done((bf16[1,64,320]{2,0,1:T(2,128)(2,1)S(1)}, bf16[1,64,320]{2,0,1:T(2,128)(2,1)S(1)}, u32[]{:S(2)}, u32[]{:S(2)}) %collective-permute-start.5) | collective-permute-done | bytes 40992 | tf_op jit(solution)/shard_map/ppermute | solution.py:19
  219.4 6.1 %collective-permute-start.6 = (bf16[18,1,320]{2,0,1:T(8,128)(2,1)S(1)}, bf16[18,1,320]{2,0,1:T(8,128)(2,1)S(1)}, u32[]{:S(2)}, u32[]{:S(2)}) collective-permute-start(bf16[18,1,320]{2,0,1:T(8,128)(2,1)S(1)} %get-tuple-element.28), channel_id=1, source_target_pairs={{0,1},{1,2},{2,3},{3,4},{4,5},{5,6},{6,7},{8,9},{9,10},{10,11},{11... | collective-permute-start | bytes 34568 | tf_op jit(solution)/shard_map/ppermute | solution.py:16
  227.5 7.4 %copy.111 = bf16[3,3,1280,160]{2,1,0,3:T(4,128)(2,1)} copy(bf16[3,3,1280,160]{2,3,1,0:T(8,128)(2,1)} %param.32) | data formatting | bytes 7372800 | tf_op args[15]
  234.9 9.4 %reshape.109 = bf16[11520,160,1]{0,1,2:T(8,128)(2,1)} reshape(bf16[3,3,1280,160]{2,1,0,3:T(4,128)(2,1)} %copy.111) | data formatting | bytes 7372800 | tf_op jit(solution)/shard_map/reshape | solution.py:63
  246.6 3.8 %convolution_select_fusion = f32[16,8,9,320]{3,1,2,0:T(8,128)S(1)} fusion(bf16[3,3,320,320]{3,2,1,0:T(8,128)(2,1)S(1)} %copy-done.16, bf16[18,1,7,2,320]{4,2,3,0,1:T(8,128)(2,1)S(1)} %slice.104, bf16[18,1,8,9,320]{4,2,3,0,1:T(8,128)(2,1)S(1)} %copy.100, pred[8,9]{0,1:T(8,128)(4,1)S(1)} %copy-done.19), kind=kOutput, calls=%fused_computation.42 | convolution fusion | flops 2126776320 | bytes 4308552 | tf_op jit(solution)/shard_map/conv_general_dilated | solution.py:25
  259.2 5.7 %fusion.45 = bf16[4,128,160]{1,2,0:T(8,128)(2,1)} fusion(bf16[4,128,11520]{2,1,0:T(8,128)(2,1)S(1)} %slice_dynamic-update-slice_fusion.3, bf16[11520,160,1]{0,1,2:T(8,128)(2,1)S(1)} %copy-done.3, f32[160]{0:T(256)S(1)} %copy-done.17, bf16[4,128,1280]{1,2,0:T(8,128)(2,1)} %copy.113, s32[]{:T(128)S(6)} %select_n.7), kind=kOutput, calls=%fused_computation.69 | convolution fusion | flops 1887764480 | bytes 15811204 | tf_op jit(solution)/shard_map/dot_general | solution.py:64
  (141 shorter events, 49.7 us)
Async XLA Ops:
  7.2 156.8 %copy-start = (bf16[3,3,320,320]{3,2,1,0:T(8,128)(2,1)S(1)}, bf16[3,3,320,320]{3,2,1,0:T(8,128)(2,1)}, u32[]{:S(2)}) copy-start(bf16[3,3,320,320]{3,2,1,0:T(8,128)(2,1)} %param.20) | copy-start | bytes 5529604
  7.2 41.1 %all-gather.3.cloned.1.call-start = ((), (), s32[]{:S(2)}) async-start(), calls=%async_computation | async-start | bytes 2211840 | tf_op jit(solution)/shard_map/all_gather | solution.py:111
  8.4 5.3 %collective-permute-start.8 = (bf16[1,16,1280]{2,1,0:T(8,128)(2,1)S(1)}, bf16[1,16,1280]{2,1,0:T(8,128)(2,1)S(1)}, u32[]{:S(2)}, u32[]{:S(2)}) collective-permute-start(bf16[1,16,1280]{2,1,0:T(8,128)(2,1)S(1)} %get-tuple-element.38), channel_id=1, source_target_pairs={{0,8},{8,16},{16,24},{1,9},{9,17},{17,25},{2,10},{10,18},{18,26},{... | collective-permute-start | bytes 122888 | tf_op jit(solution)/shard_map/ppermute | solution.py:16
  11.6 5.6 %collective-permute-start.9 = (bf16[1,16,1280]{2,1,0:T(8,128)(2,1)S(1)}, bf16[1,16,1280]{2,1,0:T(8,128)(2,1)S(1)}, u32[]{:S(2)}, u32[]{:S(2)}) collective-permute-start(bf16[1,16,1280]{2,1,0:T(8,128)(2,1)S(1)} %get-tuple-element.39), channel_id=1, source_target_pairs={{8,0},{16,8},{24,16},{9,1},{17,9},{25,17},{10,2},{18,10},{26,18},{... | collective-permute-start | bytes 122888 | tf_op jit(solution)/shard_map/ppermute | solution.py:19
  17.9 234.8 %all-gather.5.cloned.1.call-start = ((), (), s32[]{:S(2)}) async-start(), calls=%async_computation.1 | async-start | bytes 2211840 | tf_op jit(solution)/shard_map/all_gather | solution.py:123
  49.6 9.9 %copy-start.4 = (f32[1280]{0:T(1024)S(1)}, f32[1280]{0:T(1024)}, u32[]{:S(2)}) copy-start(f32[1280]{0:T(1024)} %param.28) | copy-start | bytes 15364
  49.6 10.0 %copy-start.5 = (f32[1280]{0:T(1024)S(1)}, f32[1280]{0:T(1024)}, u32[]{:S(2)}) copy-start(f32[1280]{0:T(1024)} %param.27) | copy-start | bytes 15364
  125.0 12.9 %copy-start.2 = (bf16[16,64,320]{2,1,0:T(8,128)(2,1)S(1)}, bf16[16,64,320]{2,1,0:T(8,128)(2,1)}, u32[]{:S(2)}) copy-start(bf16[16,64,320]{2,1,0:T(8,128)(2,1)} %param.17) | copy-start | bytes 1966084
  125.2 8.2 %copy-start.13 = (f32[32]{0:T(128)S(1)}, f32[32]{0:T(128)}, u32[]{:S(2)}) copy-start(f32[32]{0:T(128)} %get-tuple-element.22) | copy-start | bytes 388
  125.2 8.2 %copy-start.14 = (f32[32]{0:T(128)S(1)}, f32[32]{0:T(128)}, u32[]{:S(2)}) copy-start(f32[32]{0:T(128)} %get-tuple-element.23) | copy-start | bytes 388
  125.3 12.6 %copy-start.6 = (f32[320]{0:T(512)S(1)}, f32[320]{0:T(512)}, u32[]{:S(2)}) copy-start(f32[320]{0:T(512)} %param.19) | copy-start | bytes 3844
  125.3 12.6 %copy-start.7 = (f32[320]{0:T(512)S(1)}, f32[320]{0:T(512)}, u32[]{:S(2)}) copy-start(f32[320]{0:T(512)} %param.18) | copy-start | bytes 3844
  127.5 6.3 %collective-permute-start.10 = (bf16[1,128,160]{1,2,0:T(8,128)(2,1)S(1)}, bf16[1,128,160]{1,2,0:T(8,128)(2,1)S(1)}, u32[]{:S(2)}, u32[]{:S(2)}) collective-permute-start(bf16[1,128,160]{1,2,0:T(8,128)(2,1)S(1)} %get-tuple-element.36), channel_id=1, source_target_pairs={{0,8},{8,16},{16,24},{1,9},{9,17},{17,25},{2,10},{10,18},{18,26},{... | collective-permute-start | bytes 122888 | tf_op jit(solution)/shard_map/ppermute | solution.py:16
  131.5 5.6 %collective-permute-start.11 = (bf16[1,128,160]{1,2,0:T(8,128)(2,1)S(1)}, bf16[1,128,160]{1,2,0:T(8,128)(2,1)S(1)}, u32[]{:S(2)}, u32[]{:S(2)}) collective-permute-start(bf16[1,128,160]{1,2,0:T(8,128)(2,1)S(1)} %get-tuple-element.37), channel_id=1, source_target_pairs={{8,0},{16,8},{24,16},{9,1},{17,9},{25,17},{10,2},{18,10},{26,18},{... | collective-permute-start | bytes 122888 | tf_op jit(solution)/shard_map/ppermute | solution.py:19
  138.8 5.4 %collective-permute-start = (bf16[1,64,320]{2,0,1:T(2,128)(2,1)S(1)}, bf16[1,64,320]{2,0,1:T(2,128)(2,1)S(1)}, u32[]{:S(2)}, u32[]{:S(2)}) collective-permute-start(bf16[1,64,320]{2,0,1:T(2,128)(2,1)S(1)} %get-tuple-element.34), channel_id=1, source_target_pairs={{0,8},{8,16},{16,24},{1,9},{9,17},{17,25},{2,10},{10,18},{18,26},{... | collective-permute-start | bytes 122888 | tf_op jit(solution)/shard_map/ppermute | solution.py:16
  140.8 6.3 %collective-permute-start.1 = (bf16[1,64,320]{2,0,1:T(2,128)(2,1)S(1)}, bf16[1,64,320]{2,0,1:T(2,128)(2,1)S(1)}, u32[]{:S(2)}, u32[]{:S(2)}) collective-permute-start(bf16[1,64,320]{2,0,1:T(2,128)(2,1)S(1)} %get-tuple-element.35), channel_id=1, source_target_pairs={{8,0},{16,8},{24,16},{9,1},{17,9},{25,17},{10,2},{18,10},{26,18},{... | collective-permute-start | bytes 122888 | tf_op jit(solution)/shard_map/ppermute | solution.py:19
  147.0 11.4 %collective-permute-start.2 = (bf16[18,1,320]{2,0,1:T(8,128)(2,1)S(1)}, bf16[18,1,320]{2,0,1:T(8,128)(2,1)S(1)}, u32[]{:S(2)}, u32[]{:S(2)}) collective-permute-start(bf16[18,1,320]{2,0,1:T(8,128)(2,1)S(1)} %get-tuple-element.30), channel_id=1, source_target_pairs={{0,1},{1,2},{2,3},{3,4},{4,5},{5,6},{6,7},{8,9},{9,10},{10,11},{11... | collective-permute-start | bytes 34568 | tf_op jit(solution)/shard_map/ppermute | solution.py:16
  156.3 6.5 %collective-permute-start.3 = (bf16[18,1,320]{2,0,1:T(8,128)(2,1)S(1)}, bf16[18,1,320]{2,0,1:T(8,128)(2,1)S(1)}, u32[]{:S(2)}, u32[]{:S(2)}) collective-permute-start(bf16[18,1,320]{2,0,1:T(8,128)(2,1)S(1)} %get-tuple-element.31), channel_id=1, source_target_pairs={{1,0},{2,1},{3,2},{4,3},{5,4},{6,5},{7,6},{9,8},{10,9},{11,10},{12... | collective-permute-start | bytes 34568 | tf_op jit(solution)/shard_map/ppermute | solution.py:19
  169.4 39.9 %copy-start.8 = (f32[320]{0:T(512)S(1)}, f32[320]{0:T(512)}, u32[]{:S(2)}) copy-start(f32[320]{0:T(512)} %param.22) | copy-start | bytes 3844
  169.4 39.9 %copy-start.9 = (f32[320]{0:T(512)S(1)}, f32[320]{0:T(512)}, u32[]{:S(2)}) copy-start(f32[320]{0:T(512)} %param.21) | copy-start | bytes 3844
  210.0 5.4 %collective-permute-start.4 = (bf16[1,64,320]{2,0,1:T(2,128)(2,1)S(1)}, bf16[1,64,320]{2,0,1:T(2,128)(2,1)S(1)}, u32[]{:S(2)}, u32[]{:S(2)}) collective-permute-start(bf16[1,64,320]{2,0,1:T(2,128)(2,1)S(1)} %get-tuple-element.32), channel_id=1, source_target_pairs={{0,8},{8,16},{16,24},{1,9},{9,17},{17,25},{2,10},{10,18},{18,26},{... | collective-permute-start | bytes 122888 | tf_op jit(solution)/shard_map/ppermute | solution.py:16
  213.1 6.3 %collective-permute-start.5 = (bf16[1,64,320]{2,0,1:T(2,128)(2,1)S(1)}, bf16[1,64,320]{2,0,1:T(2,128)(2,1)S(1)}, u32[]{:S(2)}, u32[]{:S(2)}) collective-permute-start(bf16[1,64,320]{2,0,1:T(2,128)(2,1)S(1)} %get-tuple-element.33), channel_id=1, source_target_pairs={{8,0},{16,8},{24,16},{9,1},{17,9},{25,17},{10,2},{18,10},{26,18},{... | collective-permute-start | bytes 122888 | tf_op jit(solution)/shard_map/ppermute | solution.py:19
  219.4 24.9 %collective-permute-start.6 = (bf16[18,1,320]{2,0,1:T(8,128)(2,1)S(1)}, bf16[18,1,320]{2,0,1:T(8,128)(2,1)S(1)}, u32[]{:S(2)}, u32[]{:S(2)}) collective-permute-start(bf16[18,1,320]{2,0,1:T(8,128)(2,1)S(1)} %get-tuple-element.28), channel_id=1, source_target_pairs={{0,1},{1,2},{2,3},{3,4},{4,5},{5,6},{6,7},{8,9},{9,10},{10,11},{11... | collective-permute-start | bytes 34568 | tf_op jit(solution)/shard_map/ppermute | solution.py:16
  225.5 18.7 %collective-permute-start.7 = (bf16[18,1,320]{2,0,1:T(8,128)(2,1)S(1)}, bf16[18,1,320]{2,0,1:T(8,128)(2,1)S(1)}, u32[]{:S(2)}, u32[]{:S(2)}) collective-permute-start(bf16[18,1,320]{2,0,1:T(8,128)(2,1)S(1)} %get-tuple-element.29), channel_id=1, source_target_pairs={{1,0},{2,1},{3,2},{4,3},{5,4},{6,5},{7,6},{9,8},{10,9},{11,10},{12... | collective-permute-start | bytes 34568 | tf_op jit(solution)/shard_map/ppermute | solution.py:19
  (11 other events, 27.7 us)
Sparse Core Ops, SparseCore 0:
  18.1 30.1 all-gather.2
  138.0 32.4 all-gather.4
where the time goes:
time: 273 us; the launch traced here: 272 us
  blocking collectives  91.3 us (33%)
  local copies, waits for them, and re-layouts  45.5 us (17%)
  waiting for transfers between devices  45.2 us (17%)
  starting transfers between devices  41.2 us (15%)
  matrix products  18.1 us (7%)
  other arithmetic  15.6 us (6%)
  between operations  14.7 us (5%)
    psum x1, blocking collectives, body(): sums, squares = lax.psum((sums, squares), ('rows', 'cols'))  42 us
    psum x1, blocking collectives, body(): sums_two, squares_two = lax.psum((sums_two, squares_two), ('rows', 'cols'))  37.3 us
    ppermute x6, starting transfers between devices, extended(): lax.ppermute(lax.slice_in_dim(block, block.shape[dim] - width, None, axis...  27.5 us
    all_gather x1, waiting for transfers between devices, body(): whole = lax.all_gather(edged_tile, 'cols', axis=1, tiled=True)  27.1 us
    ppermute x6, waiting for transfers between devices, extended(): lax.ppermute(lax.slice_in_dim(block, 0, width, axis=dim), axis, backward)  18 us
    unnamed x52, local copies, waits for them, and re-layouts  16.6 us
    ppermute x6, starting transfers between devices, extended(): lax.ppermute(lax.slice_in_dim(block, 0, width, axis=dim), axis, backward)  13.7 us
    conv_general_dilated x3, matrix products, conv_valid(): lax.conv_general_dilated(padded[None], kernel, (1, 1), 'VALID', dimension...  12.5 us
  transfers between devices with their start and end apart: 14, of which 8 were waited for; matrix products, arithmetic and copies ran while one was open for 14% of the time, Pallas kernels for 0%

commit v1 on v0

--- a/solution.py
+++ b/solution.py
@@ -108,7 +108,7 @@
     count_three = height * width * lax.axis_size("rows") * width_three
     empty = jnp.zeros((height, width, shard), jnp.float32)
     edged_tile = extended(joined, (("rows", 0),), 1)
-    whole = lax.all_gather(edged_tile, "cols", axis=1, tiled=True)
+    whole = jnp.concatenate(lax.all_gather(edged_tile, "cols"), axis=1)
     local = lax.dynamic_slice_in_dim(whole[1:-1], lax.axis_index("cols") * shard, shard, 2)
     sums_three, squares_three = level3_totals(whole[1:-1], width_three)
     line_ids = lax.axis_index("rows") * height - 1 + jnp.arange(height + 2, dtype=jnp.int32)

time: 273 us -> 246 us (0.901)
  waiting for transfers between devices: 45.2 us -> 17.1 us
    all_gather x1, waiting for transfers between devices: 27.1 us -> 0.02 us  [body(): whole = jnp.concatenate(lax.all_gather(edged_tile, 'cols'), axis=1)]
    convert_element_type x0 -> x1, local copies, waits for them, and re-layouts: none -> 3.96 us  [normalize(): value.astype(jnp.float32).reshape(height, width, groups, chans // groups)]
    unnamed x52 -> x50, local copies, waits for them, and re-layouts: 16.6 us -> 15.1 us
  transfers between devices with their start and end apart: 14 -> 14, of which waited for: 8 -> 7; matrix products, arithmetic and copies ran while one was open for 14% -> 16% of each run, Pallas kernels for 0% -> 0%
where the time goes in v1:
time: 246 us; the launch traced here: 245 us
  blocking collectives  91.2 us (37%)
  local copies, waits for them, and re-layouts  45.8 us (19%)
  starting transfers between devices  43.6 us (18%)
  waiting for transfers between devices  17.1 us (7%)
  matrix products  17 us (7%)
  other arithmetic  15.1 us (6%)
  between operations  14.7 us (6%)
    psum x1, blocking collectives, body(): sums, squares = lax.psum((sums, squares), ('rows', 'cols'))  41.9 us
    psum x1, blocking collectives, body(): sums_two, squares_two = lax.psum((sums_two, squares_two), ('rows', 'cols'))  36.5 us
    ppermute x6, starting transfers between devices, extended(): lax.ppermute(lax.slice_in_dim(block, block.shape[dim] - width, None, axis...  30.2 us
    ppermute x6, waiting for transfers between devices, extended(): lax.ppermute(lax.slice_in_dim(block, 0, width, axis=dim), axis, backward)  16.8 us
    unnamed x50, local copies, waits for them, and re-layouts  15.1 us
    ppermute x6, starting transfers between devices, extended(): lax.ppermute(lax.slice_in_dim(block, 0, width, axis=dim), axis, backward)  13.3 us
    conv_general_dilated x3, matrix products, conv_valid(): lax.conv_general_dilated(padded[None], kernel, (1, 1), 'VALID', dimension...  12.4 us
    conv_general_dilated x11, local copies, waits for them, and re-layouts, conv_valid(): lax.conv_general_dilated(padded[None], kernel, (1, 1), 'VALID', dimension...  9.39 us
  transfers between devices with their start and end apart: 14, of which 7 were waited for; matrix products, arithmetic and copies ran while one was open for 16% of the time, Pallas kernels for 0%

profile of v1, /device:TPU:3, one launch (start us, length us, event | category | flops | bytes accessed | tf_op | source)
XLA Modules:
  0.0 244.6 jit_solution(12804370388390424686)
XLA Ops:
  8.4 3.1 %collective-permute-start.8 = (bf16[1,16,1280]{2,1,0:T(8,128)(2,1)S(1)}, bf16[1,16,1280]{2,1,0:T(8,128)(2,1)S(1)}, u32[]{:S(2)}, u32[]{:S(2)}) collective-permute-start(bf16[1,16,1280]{2,1,0:T(8,128)(2,1)S(1)} %get-tuple-element.40), channel_id=1, source_target_pairs={{0,8},{8,16},{16,24},{1,9},{9,17},{17,25},{2,10},{10,18},{18,26},{... | collective-permute-start | bytes 122888 | tf_op jit(solution)/shard_map/ppermute | solution.py:16
  13.7 3.5 %collective-permute-done.9 = bf16[1,16,1280]{2,1,0:T(8,128)(2,1)S(1)} collective-permute-done((bf16[1,16,1280]{2,1,0:T(8,128)(2,1)S(1)}, bf16[1,16,1280]{2,1,0:T(8,128)(2,1)S(1)}, u32[]{:S(2)}, u32[]{:S(2)}) %collective-permute-start.9) | collective-permute-done | bytes 40992 | tf_op jit(solution)/shard_map/ppermute | solution.py:19
  20.0 41.9 %all-reduce.3 = (f32[32]{0:T(128)S(1)}, f32[32]{0:T(128)S(1)}) all-reduce(f32[32]{0:T(128)S(1)} %reduce_sum.100, f32[32]{0:T(128)S(1)} %reduce_sum.97), channel_id=1, replica_groups=mesh['rows'=4,'cols'=8] {'rows','cols'}, use_global_device_ids=true, to_apply=%region_5.6 | all-reduce | flops 64 | bytes 512 | tf_op jit(solution)/shard_map/psum | solution.py:92
  63.9 4.0 %copy.123 = f32[6,8,16,1280]{3,2,1,0:T(8,128)} copy(bf16[6,8,16,1280]{3,2,0,1:T(8,128)(2,1)} %bitcast.80) | data formatting | bytes 5898240 | tf_op jit(solution)/shard_map/convert_element_type | solution.py:46
  68.2 6.0 %all-reduce.5 = (f32[32]{0:T(128)S(1)}, f32[32]{0:T(128)S(1)}) all-reduce(f32[32]{0:T(128)S(1)} %reduce_sum.145, f32[32]{0:T(128)S(1)} %reduce_sum.115), channel_id=1, replica_groups=mesh['rows'=4,'cols'=8] {'rows'}, use_global_device_ids=true, to_apply=%region_17.18 | all-reduce | flops 64 | bytes 512 | tf_op jit(solution)/shard_map/psum | solution.py:53
  74.6 3.5 %fusion.14 = bf16[6,128,1280]{2,1,0:T(8,128)(2,1)S(1)} fusion(f32[1280]{0:T(1024)S(1)} %copy-done.5, f32[1280]{0:T(1024)S(1)} %copy-done.6, f32[1280]{0:T(1024)S(1)} %mul.156, f32[1280]{0:T(1024)S(1)} %sub.79, f32[6,8,16,1280]{3,2,1,0:T(8,128)} %copy.123, pred[6]{0:T(512)(128)(4,1)S(1)} %compare_and_fusion), kind=kLoop, calls=%fused_computation.24 | loop fusion | flops 9830400 | bytes 5918726 | tf_op jit(solution)/shard_map/jit(_where)/select_n | solution.py:117
  80.0 4.2 %reshape.92 = bf16[6,1,8,17,1280]{4,3,2,0,1:T(8,128)(2,1)} reshape(bf16[6,1,136,1280]{3,2,0,1:T(8,128)(2,1)} %pad.13) | data formatting | bytes 4177920 | tf_op jit(solution)/shard_map/conv_general_dilated | solution.py:25
  87.1 3.5 %select_reduce_fusion.3 = (f32[160]{0:T(256)S(1)}, f32[160]{0:T(256)S(1)}, f32[4,8,17,160]{3,1,2,0:T(8,128)S(1)}) fusion(pred[8,17]{0,1:T(8,128)(4,1)S(1)} %copy-done.17, bf16[3,3,1280,160]{2,3,1,0:T(8,128)(2,1)S(1)} %copy-done.14, bf16[6,1,7,2,1280]{4,2,3,0,1:T(8,128)(2,1)S(1)} %slice.113, bf16[6,1,8,17,1280]{4,2,3,0,1:T(8,128)(2,1)S(1)} %copy.125), kind=kOutput, calls=%fused_computation.77 | convolution fusion | flops 2012927744 | bytes 6339976 | tf_op jit(solution)/shard_map/conv_general_dilated | solution.py:25
  91.2 6.9 %all-reduce.4 = (f32[4]{0:T(128)S(1)}, f32[4]{0:T(128)S(1)}) all-reduce(f32[4]{0:T(128)S(1)} %reduce_sum.151, f32[4]{0:T(128)S(1)} %reduce_sum.148), channel_id=1, replica_groups=mesh['rows'=4,'cols'=8] {'rows'}, use_global_device_ids=true, to_apply=%region_23.24 | all-reduce | flops 8 | bytes 64 | tf_op jit(solution)/shard_map/psum | solution.py:120
  99.2 3.1 %collective-permute-start.10 = (bf16[1,128,160]{1,2,0:T(8,128)(2,1)S(1)}, bf16[1,128,160]{1,2,0:T(8,128)(2,1)S(1)}, u32[]{:S(2)}, u32[]{:S(2)}) collective-permute-start(bf16[1,128,160]{1,2,0:T(8,128)(2,1)S(1)} %get-tuple-element.38), channel_id=1, source_target_pairs={{0,8},{8,16},{16,24},{1,9},{9,17},{17,25},{2,10},{10,18},{18,26},{... | collective-permute-start | bytes 122888 | tf_op jit(solution)/shard_map/ppermute | solution.py:16
  111.4 2.8 %collective-permute-start.1 = (bf16[1,64,320]{2,0,1:T(2,128)(2,1)S(1)}, bf16[1,64,320]{2,0,1:T(2,128)(2,1)S(1)}, u32[]{:S(2)}, u32[]{:S(2)}) collective-permute-start(bf16[1,64,320]{2,0,1:T(2,128)(2,1)S(1)} %get-tuple-element.37), channel_id=1, source_target_pairs={{8,0},{16,8},{24,16},{9,1},{17,9},{25,17},{10,2},{18,10},{26,18},{... | collective-permute-start | bytes 122888 | tf_op jit(solution)/shard_map/ppermute | solution.py:19
  114.3 3.3 %collective-permute-done.1 = bf16[1,64,320]{2,0,1:T(2,128)(2,1)S(1)} collective-permute-done((bf16[1,64,320]{2,0,1:T(2,128)(2,1)S(1)}, bf16[1,64,320]{2,0,1:T(2,128)(2,1)S(1)}, u32[]{:S(2)}, u32[]{:S(2)}) %collective-permute-start.1) | collective-permute-done | bytes 40992 | tf_op jit(solution)/shard_map/ppermute | solution.py:19
  117.7 11.4 %collective-permute-start.2 = (bf16[18,1,320]{2,0,1:T(8,128)(2,1)S(1)}, bf16[18,1,320]{2,0,1:T(8,128)(2,1)S(1)}, u32[]{:S(2)}, u32[]{:S(2)}) collective-permute-start(bf16[18,1,320]{2,0,1:T(8,128)(2,1)S(1)} %get-tuple-element.32), channel_id=1, source_target_pairs={{0,1},{1,2},{2,3},{3,4},{4,5},{5,6},{6,7},{8,9},{9,10},{10,11},{11... | collective-permute-start | bytes 34568 | tf_op jit(solution)/shard_map/ppermute | solution.py:16
  131.2 4.5 %collective-permute-done.3 = bf16[18,1,320]{2,0,1:T(8,128)(2,1)S(1)} collective-permute-done((bf16[18,1,320]{2,0,1:T(8,128)(2,1)S(1)}, bf16[18,1,320]{2,0,1:T(8,128)(2,1)S(1)}, u32[]{:S(2)}, u32[]{:S(2)}) %collective-permute-start.3) | collective-permute-done | bytes 11552 | tf_op jit(solution)/shard_map/ppermute | solution.py:19
  137.1 5.1 %select_reduce_fusion.1 = (f32[320]{0:T(512)S(1)}, f32[320]{0:T(512)S(1)}, f32[16,8,9,320]{3,1,2,0:T(8,128)}) fusion(pred[8,9]{0,1:T(8,128)(4,1)S(1)} %copy-done.18, bf16[3,3,320,320]{3,2,1,0:T(8,128)(2,1)S(1)} %copy-done, bf16[18,1,7,2,320]{4,2,3,0,1:T(8,128)(2,1)S(1)} %slice.104, bf16[18,1,8,9,320]{4,2,3,0,1:T(8,128)(2,1)S(1)} %copy.116), kind=kOutput, calls=%fused_computation.26 | convolution fusion | flops 2128619008 | bytes 4311112 | tf_op jit(solution)/shard_map/conv_general_dilated | solution.py:25
  142.7 36.5 %all-reduce.2 = (f32[32]{0:T(128)S(1)}, f32[32]{0:T(128)S(1)}) all-reduce(f32[32]{0:T(128)S(1)} %reduce_sum.112, f32[32]{0:T(128)S(1)} %reduce_sum.106), channel_id=1, replica_groups=mesh['rows'=4,'cols'=8] {'rows','cols'}, use_global_device_ids=true, to_apply=%region_11.12 | all-reduce | flops 64 | bytes 512 | tf_op jit(solution)/shard_map/psum | solution.py:97
  182.1 3.1 %collective-permute-start.4 = (bf16[1,64,320]{2,0,1:T(2,128)(2,1)S(1)}, bf16[1,64,320]{2,0,1:T(2,128)(2,1)S(1)}, u32[]{:S(2)}, u32[]{:S(2)}) collective-permute-start(bf16[1,64,320]{2,0,1:T(2,128)(2,1)S(1)} %get-tuple-element.34), channel_id=1, source_target_pairs={{0,8},{8,16},{16,24},{1,9},{9,17},{17,25},{2,10},{10,18},{18,26},{... | collective-permute-start | bytes 122888 | tf_op jit(solution)/shard_map/ppermute | solution.py:16
  187.5 4.0 %collective-permute-done.5 = bf16[1,64,320]{2,0,1:T(2,128)(2,1)S(1)} collective-permute-done((bf16[1,64,320]{2,0,1:T(2,128)(2,1)S(1)}, bf16[1,64,320]{2,0,1:T(2,128)(2,1)S(1)}, u32[]{:S(2)}, u32[]{:S(2)}) %collective-permute-start.5) | collective-permute-done | bytes 40992 | tf_op jit(solution)/shard_map/ppermute | solution.py:19
  191.5 6.9 %collective-permute-start.6 = (bf16[18,1,320]{2,0,1:T(8,128)(2,1)S(1)}, bf16[18,1,320]{2,0,1:T(8,128)(2,1)S(1)}, u32[]{:S(2)}, u32[]{:S(2)}) collective-permute-start(bf16[18,1,320]{2,0,1:T(8,128)(2,1)S(1)} %get-tuple-element.30), channel_id=1, source_target_pairs={{0,1},{1,2},{2,3},{3,4},{4,5},{5,6},{6,7},{8,9},{9,10},{10,11},{11... | collective-permute-start | bytes 34568 | tf_op jit(solution)/shard_map/ppermute | solution.py:16
  200.4 7.4 %copy.132 = bf16[3,3,1280,160]{2,1,0,3:T(4,128)(2,1)} copy(bf16[3,3,1280,160]{2,3,1,0:T(8,128)(2,1)} %param.32) | data formatting | bytes 7372800 | tf_op args[15]
  207.8 9.4 %reshape.122 = bf16[11520,160,1]{0,1,2:T(8,128)(2,1)} reshape(bf16[3,3,1280,160]{2,1,0,3:T(4,128)(2,1)} %copy.132) | data formatting | bytes 7372800 | tf_op jit(solution)/shard_map/reshape | solution.py:63
  219.5 3.8 %convolution_select_fusion = f32[16,8,9,320]{3,1,2,0:T(8,128)S(1)} fusion(bf16[3,3,320,320]{3,2,1,0:T(8,128)(2,1)S(1)} %copy-done.15, bf16[18,1,7,2,320]{4,2,3,0,1:T(8,128)(2,1)S(1)} %slice.108, bf16[18,1,8,9,320]{4,2,3,0,1:T(8,128)(2,1)S(1)} %copy.119, pred[8,9]{0,1:T(8,128)(4,1)S(1)} %copy-done.18), kind=kOutput, calls=%fused_computation.46 | convolution fusion | flops 2126776320 | bytes 4308552 | tf_op jit(solution)/shard_map/conv_general_dilated | solution.py:25
  226.6 2.7 %copy.128 = bf16[6,128,1280]{2,1,0:T(8,128)(2,1)S(1)} copy(bf16[6,128,1280]{1,2,0:T(8,128)(2,1)} %all-gather.4.cloned.1.call-done) | data formatting | bytes 3932160 | tf_op jit(solution)/shard_map/all_gather | solution.py:123
  233.1 4.6 %fusion.48 = bf16[4,128,160]{1,2,0:T(8,128)(2,1)} fusion(bf16[4,128,11520]{2,1,0:T(8,128)(2,1)S(1)} %slice_dynamic-update-slice_fusion.3, bf16[11520,160,1]{0,1,2:T(8,128)(2,1)S(1)} %copy-done.4, bf16[4,128,160]{1,2,0:T(8,128)(2,1)S(1)} %copy.134, f32[160]{0:T(256)S(1)} %copy-done.16), kind=kOutput, calls=%fused_computation.73 | convolution fusion | flops 1887764480 | bytes 15811200 | tf_op jit(solution)/shard_map/dot_general | solution.py:64
  (141 shorter events, 44.7 us)
Async XLA Ops:
  7.2 129.7 %copy-start = (bf16[3,3,320,320]{3,2,1,0:T(8,128)(2,1)S(1)}, bf16[3,3,320,320]{3,2,1,0:T(8,128)(2,1)}, u32[]{:S(2)}) copy-start(bf16[3,3,320,320]{3,2,1,0:T(8,128)(2,1)} %param.20) | copy-start | bytes 5529604
  7.2 55.0 %all-gather.6.cloned.1.call-start = ((), (), s32[]{:S(2)}) async-start(), calls=%async_computation.1 | async-start | bytes 2211840 | tf_op jit(solution)/shard_map/all_gather | solution.py:111
  8.4 5.3 %collective-permute-start.8 = (bf16[1,16,1280]{2,1,0:T(8,128)(2,1)S(1)}, bf16[1,16,1280]{2,1,0:T(8,128)(2,1)S(1)}, u32[]{:S(2)}, u32[]{:S(2)}) collective-permute-start(bf16[1,16,1280]{2,1,0:T(8,128)(2,1)S(1)} %get-tuple-element.40), channel_id=1, source_target_pairs={{0,8},{8,16},{16,24},{1,9},{9,17},{17,25},{2,10},{10,18},{18,26},{... | collective-permute-start | bytes 122888 | tf_op jit(solution)/shard_map/ppermute | solution.py:16
  11.6 5.6 %collective-permute-start.9 = (bf16[1,16,1280]{2,1,0:T(8,128)(2,1)S(1)}, bf16[1,16,1280]{2,1,0:T(8,128)(2,1)S(1)}, u32[]{:S(2)}, u32[]{:S(2)}) collective-permute-start(bf16[1,16,1280]{2,1,0:T(8,128)(2,1)S(1)} %get-tuple-element.41), channel_id=1, source_target_pairs={{8,0},{16,8},{24,16},{9,1},{17,9},{25,17},{10,2},{18,10},{26,18},{... | collective-permute-start | bytes 122888 | tf_op jit(solution)/shard_map/ppermute | solution.py:19
  17.9 208.7 %all-gather.4.cloned.1.call-start = ((), (), s32[]{:S(2)}) async-start(), calls=%async_computation | async-start | bytes 2211840 | tf_op jit(solution)/shard_map/all_gather | solution.py:123
  63.8 10.7 %copy-start.5 = (f32[1280]{0:T(1024)S(1)}, f32[1280]{0:T(1024)}, u32[]{:S(2)}) copy-start(f32[1280]{0:T(1024)} %param.28) | copy-start | bytes 15364
  63.8 10.7 %copy-start.6 = (f32[1280]{0:T(1024)S(1)}, f32[1280]{0:T(1024)}, u32[]{:S(2)}) copy-start(f32[1280]{0:T(1024)} %param.27) | copy-start | bytes 15364
  90.6 8.4 %copy-start.12 = (f32[160]{0:T(256)S(1)}, f32[160]{0:T(256)}, u32[]{:S(2)}) copy-start(f32[160]{0:T(256)} %param.31) | copy-start | bytes 1924
  90.6 8.4 %copy-start.13 = (f32[160]{0:T(256)S(1)}, f32[160]{0:T(256)}, u32[]{:S(2)}) copy-start(f32[160]{0:T(256)} %param.30) | copy-start | bytes 1924
  90.6 13.9 %copy-start.7 = (f32[320]{0:T(512)S(1)}, f32[320]{0:T(512)}, u32[]{:S(2)}) copy-start(f32[320]{0:T(512)} %param.19) | copy-start | bytes 3844
  90.6 13.9 %copy-start.8 = (f32[320]{0:T(512)S(1)}, f32[320]{0:T(512)}, u32[]{:S(2)}) copy-start(f32[320]{0:T(512)} %param.18) | copy-start | bytes 3844
  99.2 7.2 %collective-permute-start.10 = (bf16[1,128,160]{1,2,0:T(8,128)(2,1)S(1)}, bf16[1,128,160]{1,2,0:T(8,128)(2,1)S(1)}, u32[]{:S(2)}, u32[]{:S(2)}) collective-permute-start(bf16[1,128,160]{1,2,0:T(8,128)(2,1)S(1)} %get-tuple-element.38), channel_id=1, source_target_pairs={{0,8},{8,16},{16,24},{1,9},{9,17},{17,25},{2,10},{10,18},{18,26},{... | collective-permute-start | bytes 122888 | tf_op jit(solution)/shard_map/ppermute | solution.py:16
  102.3 5.6 %collective-permute-start.11 = (bf16[1,128,160]{1,2,0:T(8,128)(2,1)S(1)}, bf16[1,128,160]{1,2,0:T(8,128)(2,1)S(1)}, u32[]{:S(2)}, u32[]{:S(2)}) collective-permute-start(bf16[1,128,160]{1,2,0:T(8,128)(2,1)S(1)} %get-tuple-element.39), channel_id=1, source_target_pairs={{8,0},{16,8},{24,16},{9,1},{17,9},{25,17},{10,2},{18,10},{26,18},{... | collective-permute-start | bytes 122888 | tf_op jit(solution)/shard_map/ppermute | solution.py:19
  108.9 5.4 %collective-permute-start = (bf16[1,64,320]{2,0,1:T(2,128)(2,1)S(1)}, bf16[1,64,320]{2,0,1:T(2,128)(2,1)S(1)}, u32[]{:S(2)}, u32[]{:S(2)}) collective-permute-start(bf16[1,64,320]{2,0,1:T(2,128)(2,1)S(1)} %get-tuple-element.36), channel_id=1, source_target_pairs={{0,8},{8,16},{16,24},{1,9},{9,17},{17,25},{2,10},{10,18},{18,26},{... | collective-permute-start | bytes 122888 | tf_op jit(solution)/shard_map/ppermute | solution.py:16
  111.4 6.3 %collective-permute-start.1 = (bf16[1,64,320]{2,0,1:T(2,128)(2,1)S(1)}, bf16[1,64,320]{2,0,1:T(2,128)(2,1)S(1)}, u32[]{:S(2)}, u32[]{:S(2)}) collective-permute-start(bf16[1,64,320]{2,0,1:T(2,128)(2,1)S(1)} %get-tuple-element.37), channel_id=1, source_target_pairs={{8,0},{16,8},{24,16},{9,1},{17,9},{25,17},{10,2},{18,10},{26,18},{... | collective-permute-start | bytes 122888 | tf_op jit(solution)/shard_map/ppermute | solution.py:19
  117.7 13.5 %collective-permute-start.2 = (bf16[18,1,320]{2,0,1:T(8,128)(2,1)S(1)}, bf16[18,1,320]{2,0,1:T(8,128)(2,1)S(1)}, u32[]{:S(2)}, u32[]{:S(2)}) collective-permute-start(bf16[18,1,320]{2,0,1:T(8,128)(2,1)S(1)} %get-tuple-element.32), channel_id=1, source_target_pairs={{0,1},{1,2},{2,3},{3,4},{4,5},{5,6},{6,7},{8,9},{9,10},{10,11},{11... | collective-permute-start | bytes 34568 | tf_op jit(solution)/shard_map/ppermute | solution.py:16
  129.1 6.6 %collective-permute-start.3 = (bf16[18,1,320]{2,0,1:T(8,128)(2,1)S(1)}, bf16[18,1,320]{2,0,1:T(8,128)(2,1)S(1)}, u32[]{:S(2)}, u32[]{:S(2)}) collective-permute-start(bf16[18,1,320]{2,0,1:T(8,128)(2,1)S(1)} %get-tuple-element.33), channel_id=1, source_target_pairs={{1,0},{2,1},{3,2},{4,3},{5,4},{6,5},{7,6},{9,8},{10,9},{11,10},{12... | collective-permute-start | bytes 34568 | tf_op jit(solution)/shard_map/ppermute | solution.py:19
  142.3 39.1 %copy-start.9 = (f32[320]{0:T(512)S(1)}, f32[320]{0:T(512)}, u32[]{:S(2)}) copy-start(f32[320]{0:T(512)} %param.22) | copy-start | bytes 3844
  142.3 39.1 %copy-start.10 = (f32[320]{0:T(512)S(1)}, f32[320]{0:T(512)}, u32[]{:S(2)}) copy-start(f32[320]{0:T(512)} %param.21) | copy-start | bytes 3844
  182.1 5.4 %collective-permute-start.4 = (bf16[1,64,320]{2,0,1:T(2,128)(2,1)S(1)}, bf16[1,64,320]{2,0,1:T(2,128)(2,1)S(1)}, u32[]{:S(2)}, u32[]{:S(2)}) collective-permute-start(bf16[1,64,320]{2,0,1:T(2,128)(2,1)S(1)} %get-tuple-element.34), channel_id=1, source_target_pairs={{0,8},{8,16},{16,24},{1,9},{9,17},{17,25},{2,10},{10,18},{18,26},{... | collective-permute-start | bytes 122888 | tf_op jit(solution)/shard_map/ppermute | solution.py:16
  185.2 6.3 %collective-permute-start.5 = (bf16[1,64,320]{2,0,1:T(2,128)(2,1)S(1)}, bf16[1,64,320]{2,0,1:T(2,128)(2,1)S(1)}, u32[]{:S(2)}, u32[]{:S(2)}) collective-permute-start(bf16[1,64,320]{2,0,1:T(2,128)(2,1)S(1)} %get-tuple-element.35), channel_id=1, source_target_pairs={{8,0},{16,8},{24,16},{9,1},{17,9},{25,17},{10,2},{18,10},{26,18},{... | collective-permute-start | bytes 122888 | tf_op jit(solution)/shard_map/ppermute | solution.py:19
  191.5 25.7 %collective-permute-start.6 = (bf16[18,1,320]{2,0,1:T(8,128)(2,1)S(1)}, bf16[18,1,320]{2,0,1:T(8,128)(2,1)S(1)}, u32[]{:S(2)}, u32[]{:S(2)}) collective-permute-start(bf16[18,1,320]{2,0,1:T(8,128)(2,1)S(1)} %get-tuple-element.30), channel_id=1, source_target_pairs={{0,1},{1,2},{2,3},{3,4},{4,5},{5,6},{6,7},{8,9},{9,10},{10,11},{11... | collective-permute-start | bytes 34568 | tf_op jit(solution)/shard_map/ppermute | solution.py:16
  198.4 18.7 %collective-permute-start.7 = (bf16[18,1,320]{2,0,1:T(8,128)(2,1)S(1)}, bf16[18,1,320]{2,0,1:T(8,128)(2,1)S(1)}, u32[]{:S(2)}, u32[]{:S(2)}) collective-permute-start(bf16[18,1,320]{2,0,1:T(8,128)(2,1)S(1)} %get-tuple-element.31), channel_id=1, source_target_pairs={{1,0},{2,1},{3,2},{4,3},{5,4},{6,5},{7,6},{9,8},{10,9},{11,10},{12... | collective-permute-start | bytes 34568 | tf_op jit(solution)/shard_map/ppermute | solution.py:19
  233.1 4.6 %copy-start.1 = (bf16[3,3,320,320]{3,2,1,0:T(8,128)(2,1)S(1)}, bf16[3,3,320,320]{3,2,1,0:T(8,128)(2,1)}, u32[]{:S(2)}) copy-start(bf16[3,3,320,320]{3,2,1,0:T(8,128)(2,1)} %param.20) | copy-start | bytes 5529604
  (9 other events, 16.1 us)
Sparse Core Ops, SparseCore 0:
  18.1 30.8 all-gather.5
  108.9 33.7 all-gather.3
